TPU v7x, 32 devices: a whole 2x2x4 slice. The times are simulated.
32 devices in a mesh: obs: 8 (over z, x), bel: 4 (over y, core).
Axes of the slice: x: 2, y: 2, z: 4, core: 2. Of those that a mesh axis runs over, the one named last changes fastest.
Arguments:
- alpha_set: bfloat16 [2048, 2048], P('bel'), may hold values from -600 to 600
- transitions: bfloat16 [16, 2048, 2048], P(None, 'obs'), may hold values from 0.0009994507 to 1
- obs_weights: float32 [256, 16, 2048], P('obs'), may hold values from 0.01 to 1
- rewards: float32 [16, 2048], replicated, may hold values from -1 to 1
- chosen_idx: int32 [1536, 16, 256], P('bel', None, 'obs'), may hold values from 0 to 2047
- chosen_action: int32 [1536], P('bel'), may hold values from 0 to 15
Outputs:
- new_alpha: float32 [1536, 2048], P(('bel', 'obs'))
Inputs may be any that keep to these rules, and one draw needn't show every extreme that they name: `chosen_idx`: an index into the 2048 alpha vectors. `chosen_action`: an index into the 16 actions.
All inputs are finite; a program needn't handle non-finite values.
Results may differ from a plain program's by a relative error of at most 0.0003.
Values may be sent and summed in bfloat16 or wider, within the bound.
A program may use at most 192 MiB of HBM per device.

v0:
```python
import jax
import jax.numpy as jnp
from jax import lax
from jax.sharding import PartitionSpec as P

discount = 0.95


def action_table(actions, count):
    return (actions[:, None] == jnp.arange(count, dtype=jnp.int32)[None, :]).astype(jnp.float32)


def picked_rows(indices, hot):
    chosen = jnp.sum(jnp.where(hot[:, :, None] > 0, indices, 0), axis=1)
    return chosen.T


def body(alpha_set, transitions, obs_weights, rewards, chosen_idx, chosen_action):
    actions = rewards.shape[0]
    states = rewards.shape[1]
    obs_local = obs_weights.shape[0]
    bel_rows = chosen_action.shape[0]
    trans_raw = transitions.astype(jnp.float32)
    action_hot = action_table(chosen_action, actions)
    picks = picked_rows(chosen_idx, action_hot).reshape(-1)
    piece = lax.all_gather(alpha_set, "bel", axis=0, tiled=True)
    count = piece.shape[0]
    onehot = (picks[:, None] == jnp.arange(count, dtype=jnp.int32)[None, :]).astype(jnp.bfloat16)
    chosen = jnp.dot(onehot, piece, preferred_element_type=jnp.float32)
    chosen = chosen.reshape(obs_local, bel_rows, states)
    obs_totals, trans_totals = lax.psum(
        (jnp.sum(obs_weights, axis=0), jnp.sum(trans_raw, axis=1)), "obs"
    )
    obs_prob = obs_weights / obs_totals[None, :, :]
    belief_prob = jnp.einsum("ba,oas->obs", action_hot, obs_prob, precision=lax.Precision.HIGHEST)
    partial_value = jnp.sum(belief_prob * chosen, axis=0)
    slice_w = lax.psum_scatter(partial_value, "obs", scatter_dimension=1, tiled=True)
    trans_prob = trans_raw / trans_totals[:, None, :]
    width = slice_w.shape[1]
    spread = (action_hot[:, :, None] * slice_w[:, None, :]).reshape(bel_rows, actions * width)
    table = trans_prob.reshape(actions * width, states)
    owned = bel_rows // lax.axis_size("obs")
    future = lax.psum_scatter(
        jnp.dot(spread, table, precision=lax.Precision.HIGHEST, preferred_element_type=jnp.float32),
        "obs",
        scatter_dimension=0,
        tiled=True,
    )
    own_hot = lax.dynamic_slice_in_dim(action_hot, lax.axis_index("obs") * owned, owned, 0)
    reward_rows = jnp.dot(
        own_hot, rewards, precision=lax.Precision.HIGHEST, preferred_element_type=jnp.float32
    )
    return reward_rows + discount * future


def solution(mesh):
    placed = (
        P("bel", None),
        P(None, "obs", None),
        P("obs", None, None),
        P(),
        P("bel", None, "obs"),
        P("bel"),
    )
    return jax.shard_map(
        body, mesh=mesh, in_specs=placed, out_specs=P(("bel", "obs"), None), check_vma=False
    )
```

profile of v0, /device:TPU:0, one launch (start us, length us, event | category | flops | bytes accessed | tf_op | source)
XLA Modules:
  0.0 457.6 jit_solution(5669605454711230280)
XLA Ops:
  7.4 0.0 copy-start
  7.4 0.0 all-gather.2.cloned.1.call-start
  7.4 0.7 all-gather.2.cloned.1.call-update
  8.1 0.0 all-reduce.3.cloned.1.call-start
  8.1 3.0 reduce_sum.36
  11.2 0.0 copy-start.3
  11.2 0.0 copy-start.1
  11.2 7.7 %convert_reduce_fusion = f32[16,2048]{1,0:T(8,128)} fusion(bf16[16,256,2048]{2,1,0:T(8,128)(2,1)} %param.7), kind=kLoop, calls=%fused_computation.6 | loop fusion | flops 16744448 | bytes 16908288 | tf_op jit(solution)/shard_map/reduce_sum | solution.py:32
  18.9 0.0 all-reduce.3.cloned.1.call-update
  18.9 0.0 reduce-scatter.3.cloned.1.call-start
  19.0 0.0 copy-done.3
  19.0 0.6 iota_compare_fusion.2
  19.6 0.0 copy-done.1
  19.6 0.1 select_reduce_fusion
  19.7 51.1 %all-gather.2.cloned.1.call-done = bf16[2048,2048]{1,0:T(8,128)(2,1)} async-done(((bf16[512,2048]{1,0:T(8,128)(2,1)}), bf16[2048,2048]{1,0:T(8,128)(2,1)}) %all-gather.2.cloned.1.call-update) | async-done | bytes 8388624 | tf_op jit(solution)/shard_map/all_gather | solution.py:26
  70.7 0.0 copy-start.4
  70.8 116.2 %fusion.1 = f32[12288,2048]{1,0:T(8,128)} fusion(bf16[2048,2048]{1,0:T(8,128)(2,1)} %all-gather.2.cloned.1.call-done, s32[12288]{0:T(1024)S(1)} %eq.38), kind=kOutput, calls=%fused_computation.3 | convolution fusion | flops 103104380928 | bytes 109101056 | tf_op jit(solution)/shard_map/dot_general | solution.py:29
  187.0 0.0 all-reduce.3.cloned.1.call-done
  187.0 0.0 copy-done.4
  187.0 0.0 copy-start.2
  187.0 62.6 %fusion = f32[384,2048]{1,0:T(8,128)} fusion(f32[32,384,2048]{2,1,0:T(8,128)} %bitcast.3, f32[32,16,2048]{2,1,0:T(8,128)} %param.8, f32[16,2048]{1,0:T(8,128)} %get-tuple-element.6, s32[384]{0:T(512)S(1)} %copy-done.4), kind=kOutput, calls=%fused_computation.1 | convolution fusion | flops 4882438144 | bytes 108135936 | tf_op jit(solution)/shard_map/ba,oas->obs/dot_general | solution.py:35
  249.6 0.0 copy-start.5
  249.6 0.0 reduce-scatter.3.cloned.1.call-update
  249.6 0.0 reduce-scatter.5.cloned.1.call-start
  249.6 75.1 %reduce-scatter.3.cloned.1.call-done = f32[384,256]{1,0:T(8,128)} async-done(((f32[384,2048]{1,0:T(8,128)}), f32[384,256]{1,0:T(8,128)}) %reduce-scatter.3.cloned.1.call-update) | async-done | bytes 393232 | tf_op jit(solution)/shard_map/reduce_scatter | solution.py:37
  324.8 0.0 copy-done.2
  324.8 1.9 fusion.30
  326.6 0.0 copy-done.5
  326.6 47.3 %fusion.9 = f32[384,2048]{1,0:T(8,128)} fusion(bf16[16,256,2048]{2,1,0:T(8,128)(2,1)} %param.7, f32[16,2048]{1,0:T(8,128)S(1)} %copy-done.5, f32[384,16,256]{2,0,1:T(8,128)S(1)} %fusion.30), kind=kOutput, calls=%fused_computation.13 | convolution fusion | flops 38671482880 | bytes 26345472 | tf_op jit(solution)/shard_map/dot_general | solution.py:44
  373.9 0.0 reduce-scatter.5.cloned.1.call-update
  374.0 73.8 %reduce-scatter.5.cloned.1.call-done = f32[48,2048]{1,0:T(8,128)} async-done(((f32[384,2048]{1,0:T(8,128)}), f32[48,2048]{1,0:T(8,128)}) %reduce-scatter.5.cloned.1.call-update) | async-done | bytes 393232 | tf_op jit(solution)/shard_map/reduce_scatter | solution.py:43
  447.8 0.0 copy-done
  447.8 2.2 convolution_add_fusion
  (1 shorter events, 0.0 us)
Async XLA Ops:
  7.4 440.4 %copy-start = (f32[16,2048]{1,0:T(8,128)S(1)}, f32[16,2048]{1,0:T(8,128)}, u32[]{:S(2)}) copy-start(f32[16,2048]{1,0:T(8,128)} %param.9) | copy-start | bytes 393220
  7.4 63.4 %all-gather.2.cloned.1.call-start = ((), (), s32[]{:S(2)}) async-start(), calls=%async_computation.2 | async-start | bytes 10485760 | tf_op jit(solution)/shard_map/all_gather | solution.py:26
  8.1 178.9 %all-reduce.3.cloned.1.call-start = ((), (), s32[]{:S(2)}) async-start(), calls=%async_computation.5 | async-start | bytes 524288 | tf_op jit(solution)/shard_map/psum | solution.py:31
  11.2 7.8 %copy-start.3 = (s32[384]{0:T(512)S(1)}, s32[384]{0:T(512)}, u32[]{:S(2)}) copy-start(s32[384]{0:T(512)} %param.11) | copy-start | bytes 4612
  11.2 8.4 %copy-start.1 = (s32[384,16,32]{0,2,1:T(8,128)S(1)}, s32[384,16,32]{0,2,1:T(8,128)}, u32[]{:S(2)}) copy-start(s32[384,16,32]{0,2,1:T(8,128)} %param.10) | copy-start | bytes 2359300
  18.9 305.8 %reduce-scatter.3.cloned.1.call-start = ((), (), s32[]{:S(2)}) async-start(), calls=%async_computation.3 | async-start | bytes 3538944 | tf_op jit(solution)/shard_map/reduce_scatter | solution.py:37
  70.7 116.2 %copy-start.4 = (s32[384]{0:T(512)S(1)}, s32[384]{0:T(512)}, u32[]{:S(2)}) copy-start(s32[384]{0:T(512)} %param.11) | copy-start | bytes 4612
  187.0 137.8 %copy-start.2 = (f32[384,16]{0,1:T(8,128)S(1)}, f32[384,16]{0,1:T(8,128)}, u32[]{:S(2)}) copy-start(f32[384,16]{0,1:T(8,128)} %get-tuple-element.9) | copy-start | bytes 73732
  249.6 77.1 %copy-start.5 = (f32[16,2048]{1,0:T(8,128)S(1)}, f32[16,2048]{1,0:T(8,128)}, u32[]{:S(2)}) copy-start(f32[16,2048]{1,0:T(8,128)} %get-tuple-element.5) | copy-start | bytes 393220
  249.6 198.2 %reduce-scatter.5.cloned.1.call-start = ((), (), s32[]{:S(2)}) async-start(), calls=%async_computation.4 | async-start | bytes 3538944 | tf_op jit(solution)/shard_map/reduce_scatter | solution.py:43
Sparse Core Ops, SparseCore 0:
  9.7 60.9 all-gather.1
Sparse Core Ops, SparseCore 1:
  19.0 74.0 all-reduce.2
  249.7 75.0 reduce-scatter.2
  374.1 73.7 reduce-scatter.4
where the time goes:
time: 458 us
  matrix products  228 us (50%)
  waiting for transfers between devices  201 us (44%)
  between operations  15.1 us (3%)
  other arithmetic  13.3 us (3%)
    dot_general x1, matrix products, body(): chosen = jnp.dot(onehot, piece, preferred_element_type=jnp.float32)  116 us
    reduce_scatter x1, waiting for transfers between devices, body(): lax.psum_scatter(partial_value, 'obs', scatter_dimension=1, tiled=True)  75.1 us
    reduce_scatter x1, waiting for transfers between devices, body(): lax.psum_scatter(jnp.dot(spread, table, precision=lax.Precision.HIGHEST,...  73.8 us
    dot_general x1, matrix products, body(): jnp.einsum('ba,oas->obs', action_hot, obs_prob, precision=lax.Precision.H...  62.6 us
    all_gather x1, waiting for transfers between devices, body(): piece = lax.all_gather(alpha_set, 'bel', axis=0, tiled=True)  51.1 us
    dot_general x1, matrix products, body(): jnp.dot(spread, table, precision=lax.Precision.HIGHEST, preferred_element...  47.3 us
  transfers between devices with their start and end apart: 4, of which 3 were waited for; matrix products, arithmetic and copies ran while one was open for 28% of the time, Pallas kernels for 0%

commit v1 on v0

--- a/solution.py
+++ b/solution.py
@@ -4,6 +4,28 @@
 from jax.sharding import PartitionSpec as P
 
 discount = 0.95
+
+
+def laid_out(parts, dim):
+    lengths = list(parts.shape[1:])
+    lengths[dim] *= parts.shape[0]
+    return jnp.moveaxis(parts, 0, dim).reshape(lengths)
+
+
+def collect(value, axis, dim):
+    size = lax.axis_size(axis)
+    pairs = [(i, (i + 1) % size) for i in range(size)]
+    back = [(b, a) for a, b in pairs]
+    lower, upper = ([], [])
+    for step in range(size - 1):
+        if step % 2 == 0:
+            lower.append(lax.ppermute(lower[-1] if lower else value, axis, pairs))
+        else:
+            upper.append(lax.ppermute(upper[-1] if upper else value, axis, back))
+    pieces = jnp.stack([*lower[::-1], value, *upper])
+    shift = lax.axis_index(axis) - len(lower)
+    pieces = pieces[(jnp.arange(size) - shift) % size]
+    return laid_out(pieces, dim)
 
 
 def action_table(actions, count):
@@ -23,7 +45,7 @@
     trans_raw = transitions.astype(jnp.float32)
     action_hot = action_table(chosen_action, actions)
     picks = picked_rows(chosen_idx, action_hot).reshape(-1)
-    piece = lax.all_gather(alpha_set, "bel", axis=0, tiled=True)
+    piece = collect(alpha_set, "bel", 0)
     count = piece.shape[0]
     onehot = (picks[:, None] == jnp.arange(count, dtype=jnp.int32)[None, :]).astype(jnp.bfloat16)
     chosen = jnp.dot(onehot, piece, preferred_element_type=jnp.float32)

time: 458 us -> 504 us (1.10)
  waiting for transfers between devices: 201 us -> 217 us
  local copies, waits for them, and re-layouts: 0.03 us -> 14.7 us
  other arithmetic: 13.3 us -> 23.9 us
    all_gather x1 -> x0, waiting for transfers between devices: 51.1 us -> none  [body(): piece = lax.all_gather(alpha_set, 'bel', axis=0, tiled=True)]
    psum x1, waiting for transfers between devices: 0.01 us -> 37.9 us  [body(): lax.psum((jnp.sum(obs_weights, axis=0), jnp.sum(trans_raw, axis=1)), 'obs')]
    ppermute x0 -> x3, waiting for transfers between devices: none -> 32.2 us  [the longest x2 32.2 us: collect(): lower.append(lax.ppermute(lower[-1] if lower else value, axis, pairs))]
    dot_general x1, matrix products: 116 us -> 133 us  [body(): chosen = jnp.dot(onehot, piece, preferred_element_type=jnp.float32)]
    dot_general x1, matrix products: 62.6 us -> 47.1 us  [body(): jnp.einsum('ba,oas->obs', action_hot, obs_prob, precision=lax.Precision.H...]
    gather x0 -> x3, local copies, waits for them, and re-layouts: none -> 13.5 us  [collect(): pieces = pieces[(jnp.arange(size) - shift) % size]]
    unnamed x0 -> x1, other arithmetic: none -> 8.24 us
    ppermute x0 -> x3, starting transfers between devices: none -> 5.06 us  [the longest x2 3.12 us: collect(): lower.append(lax.ppermute(lower[-1] if lower else value, axis, pairs))]
  transfers between devices with their start and end apart: 4 -> 6, of which waited for: 3 -> 4; matrix products, arithmetic and copies ran while one was open for 28% -> 12% of each run, Pallas kernels for 0% -> 0%
where the time goes in v1:
time: 504 us
  matrix products  229 us (45%)
  waiting for transfers between devices  217 us (43%)
  other arithmetic  23.9 us (5%)
  local copies, waits for them, and re-layouts  14.7 us (3%)
  between operations  13.2 us (3%)
  starting transfers between devices  5.14 us (1%)
    dot_general x1, matrix products, body(): chosen = jnp.dot(onehot, piece, preferred_element_type=jnp.float32)  133 us
    reduce_scatter x1, waiting for transfers between devices, body(): lax.psum_scatter(partial_value, 'obs', scatter_dimension=1, tiled=True)  73.7 us
    reduce_scatter x1, waiting for transfers between devices, body(): lax.psum_scatter(jnp.dot(spread, table, precision=lax.Precision.HIGHEST,...  73.5 us
    dot_general x1, matrix products, body(): jnp.dot(spread, table, precision=lax.Precision.HIGHEST, preferred_element...  47.3 us
    dot_general x1, matrix products, body(): jnp.einsum('ba,oas->obs', action_hot, obs_prob, precision=lax.Precision.H...  47.1 us
    psum x1, waiting for transfers between devices, body(): lax.psum((jnp.sum(obs_weights, axis=0), jnp.sum(trans_raw, axis=1)), 'obs')  37.9 us
    ppermute x2, waiting for transfers between devices, collect(): lower.append(lax.ppermute(lower[-1] if lower else value, axis, pairs))  32.2 us
    gather x3, local copies, waits for them, and re-layouts, collect(): pieces = pieces[(jnp.arange(size) - shift) % size]  13.5 us
  transfers between devices with their start and end apart: 6, of which 4 were waited for; matrix products, arithmetic and copies ran while one was open for 12% of the time, Pallas kernels for 0%

profile of v1, /device:TPU:0, one launch (start us, length us, event | category | flops | bytes accessed | tf_op | source)
XLA Modules:
  0.0 503.6 jit_solution(16297428703179448242)
XLA Ops:
  6.5 0.0 copy-start
  6.5 0.0 all-reduce.3.cloned.1.call-start
  6.5 0.5 collective-permute-start
  7.0 1.9 collective-permute-start.2
  9.0 3.0 reduce_sum.36
  12.0 0.0 copy-start.4
  12.0 0.0 copy-start.2
  12.0 7.7 %convert_reduce_fusion = f32[16,2048]{1,0:T(8,128)} fusion(bf16[16,256,2048]{2,1,0:T(8,128)(2,1)} %param.7), kind=kLoop, calls=%fused_computation.9 | loop fusion | flops 16744448 | bytes 16908288 | tf_op jit(solution)/shard_map/reduce_sum | solution.py:54
  19.7 0.0 all-reduce.3.cloned.1.call-update
  19.8 0.0 reduce-scatter.3.cloned.1.call-start
  19.8 0.0 copy-done.4
  19.8 0.6 iota_compare_fusion.1
  20.5 0.0 copy-done.2
  20.5 0.1 select_reduce_fusion
  20.6 32.2 %collective-permute-done = bf16[512,2048]{1,0:T(8,128)(2,1)S(1)} collective-permute-done((bf16[512,2048]{1,0:T(8,128)(2,1)}, bf16[512,2048]{1,0:T(8,128)(2,1)S(1)}, u32[]{:S(2)}, u32[]{:S(2)}) %collective-permute-start) | collective-permute-done | bytes 2097184 | tf_op jit(solution)/shard_map/ppermute | solution.py:22
  52.8 2.6 collective-permute-start.1
  55.4 37.9 %all-reduce.3.cloned.1.call-done = (f32[16,2048]{1,0:T(8,128)}, f32[16,2048]{1,0:T(8,128)}) async-done(((f32[16,2048]{1,0:T(8,128)}, f32[16,2048]{1,0:T(8,128)}), (f32[16,2048]{1,0:T(8,128)}, f32[16,2048]{1,0:T(8,128)})) %all-reduce.3.cloned.1.call-update) | async-done | bytes 262160 | tf_op jit(solution)/shard_map/psum | solution.py:53
  93.3 0.0 copy-start.1
  93.3 47.1 %fusion.10 = f32[32,2048,384]{2,1,0:T(8,128)} fusion(f32[32,16,2048]{2,1,0:T(8,128)} %param.8, f32[16,2048]{1,0:T(8,128)} %get-tuple-element.6, s32[384]{0:T(512)S(1)} %copy-done.4), kind=kOutput, calls=%fused_computation.15 | convolution fusion | flops 4832892928 | bytes 104990208 | tf_op jit(solution)/shard_map/ba,oas->obs/dot_general | solution.py:57
  140.4 0.0 collective-permute-done.2
  140.4 0.0 collective-permute-done.1
  140.4 0.0 copy-done.1
  140.4 3.3 pad_maximum_fusion
  143.7 3.7 fusion.25
  147.4 4.9 gather_fusion
  152.4 4.9 gather_fusion.1
  157.3 8.2 %pad_maximum_fusion.1 = bf16[4,512,2048]{2,1,0:T(8,128)(2,1)} fusion(bf16[4,512,1024]{2,1,0:T(8,128)(2,1)} %gather_fusion.1, bf16[4,512,1024]{2,1,0:T(8,128)(2,1)} %gather_fusion), kind=kLoop, calls=%fused_computation.13 | loop fusion | flops 16777216 | bytes 16777216
  165.5 0.0 copy-start.3
  165.5 132.7 %fusion = f32[384,2048]{0,1:T(8,128)} fusion(f32[32,2048,384]{2,1,0:T(8,128)} %fusion.10, bf16[2048,2048,1]{1,0,2:T(8,128)(2,1)} %bitcast.36, s32[32,384]{1,0:T(8,128)S(1)} %bitcast.39), kind=kOutput, calls=%fused_computation.3 | convolution fusion | flops 103153926144 | bytes 112246784 | tf_op jit(solution)/shard_map/dot_general | solution.py:51
  298.3 0.0 copy-start.5
  298.3 0.0 reduce-scatter.3.cloned.1.call-update
  298.3 0.0 reduce-scatter.5.cloned.1.call-start
  298.4 73.7 %reduce-scatter.3.cloned.1.call-done = f32[384,256]{0,1:T(8,128)} async-done(((f32[384,2048]{0,1:T(8,128)}), f32[384,256]{0,1:T(8,128)}) %reduce-scatter.3.cloned.1.call-update) | async-done | bytes 393232 | tf_op jit(solution)/shard_map/reduce_scatter | solution.py:59
  372.0 1.2 copy.9
  373.2 0.0 copy-done.3
  373.2 0.9 fusion.40
  374.1 0.0 copy-done.5
  374.1 47.3 %fusion.14 = f32[384,2048]{1,0:T(8,128)} fusion(bf16[16,256,2048]{2,1,0:T(8,128)(2,1)} %param.7, f32[16,2048]{1,0:T(8,128)S(1)} %copy-done.5, f32[384,16,256]{2,0,1:T(8,128)S(1)} %fusion.40), kind=kOutput, calls=%fused_computation.19 | convolution fusion | flops 38671482880 | bytes 26345472 | tf_op jit(solution)/shard_map/dot_general | solution.py:66
  421.4 0.0 reduce-scatter.5.cloned.1.call-update
  421.4 73.5 %reduce-scatter.5.cloned.1.call-done = f32[48,2048]{1,0:T(8,128)} async-done(((f32[384,2048]{1,0:T(8,128)}), f32[48,2048]{1,0:T(8,128)}) %reduce-scatter.5.cloned.1.call-update) | async-done | bytes 393232 | tf_op jit(solution)/shard_map/reduce_scatter | solution.py:65
  494.9 0.0 copy-done
  494.9 2.2 convolution_add_fusion
  (2 shorter events, 0.0 us)
Async XLA Ops:
  6.5 488.4 %copy-start = (f32[16,2048]{1,0:T(8,128)S(1)}, f32[16,2048]{1,0:T(8,128)}, u32[]{:S(2)}) copy-start(f32[16,2048]{1,0:T(8,128)} %param.9) | copy-start | bytes 393220
  6.5 86.8 %all-reduce.3.cloned.1.call-start = ((), (), s32[]{:S(2)}) async-start(), calls=%async_computation.4 | async-start | bytes 524288 | tf_op jit(solution)/shard_map/psum | solution.py:53
  6.5 46.2 %collective-permute-start = (bf16[512,2048]{1,0:T(8,128)(2,1)}, bf16[512,2048]{1,0:T(8,128)(2,1)S(1)}, u32[]{:S(2)}, u32[]{:S(2)}) collective-permute-start(bf16[512,2048]{1,0:T(8,128)(2,1)} %param.6), channel_id=1, source_target_pairs={{0,1},{1,2},{2,3},{3,0},{4,5},{5,6},{6,7},{7,4},{8,9},{9,10},{10,1... | collective-permute-start | bytes 6291464 | tf_op jit(solution)/shard_map/ppermute | solution.py:22
  7.0 133.3 %collective-permute-start.2 = (bf16[512,2048]{1,0:T(8,128)(2,1)}, bf16[512,2048]{1,0:T(8,128)(2,1)}, u32[]{:S(2)}, u32[]{:S(2)}) collective-permute-start(bf16[512,2048]{1,0:T(8,128)(2,1)} %param.6), channel_id=1, source_target_pairs={{1,0},{2,1},{3,2},{0,3},{5,4},{6,5},{7,6},{4,7},{9,8},{10,9},{11,1... | collective-permute-start | bytes 6291464 | tf_op jit(solution)/shard_map/ppermute | solution.py:24
  12.0 7.8 %copy-start.4 = (s32[384]{0:T(512)S(1)}, s32[384]{0:T(512)}, u32[]{:S(2)}) copy-start(s32[384]{0:T(512)} %param.11) | copy-start | bytes 4612
  12.0 8.4 %copy-start.2 = (s32[384,16,32]{0,2,1:T(8,128)S(1)}, s32[384,16,32]{0,2,1:T(8,128)}, u32[]{:S(2)}) copy-start(s32[384,16,32]{0,2,1:T(8,128)} %param.10) | copy-start | bytes 2359300
  19.8 352.3 %reduce-scatter.3.cloned.1.call-start = ((), (), s32[]{:S(2)}) async-start(), calls=%async_computation.2 | async-start | bytes 3538944 | tf_op jit(solution)/shard_map/reduce_scatter | solution.py:59
  52.8 87.6 %collective-permute-start.1 = (bf16[512,2048]{1,0:T(8,128)(2,1)S(1)}, bf16[512,2048]{1,0:T(8,128)(2,1)}, u32[]{:S(2)}, u32[]{:S(2)}) collective-permute-start(bf16[512,2048]{1,0:T(8,128)(2,1)S(1)} %collective-permute-done), channel_id=1, source_target_pairs={{0,1},{1,2},{2,3},{3,0},{4,5},{5,6},{6,7},{7,4},{8,9},{9,10},{10,1... | collective-permute-start | bytes 6291464 | tf_op jit(solution)/shard_map/ppermute | solution.py:22
  93.3 47.1 %copy-start.1 = (bf16[512,2048]{1,0:T(8,128)(2,1)S(1)}, bf16[512,2048]{1,0:T(8,128)(2,1)}, u32[]{:S(2)}) copy-start(bf16[512,2048]{1,0:T(8,128)(2,1)} %param.6) | copy-start | bytes 6291460
  165.5 207.7 %copy-start.3 = (f32[384,16]{0,1:T(8,128)S(1)}, f32[384,16]{0,1:T(8,128)}, u32[]{:S(2)}) copy-start(f32[384,16]{0,1:T(8,128)} %get-tuple-element.11) | copy-start | bytes 73732
  298.3 75.8 %copy-start.5 = (f32[16,2048]{1,0:T(8,128)S(1)}, f32[16,2048]{1,0:T(8,128)}, u32[]{:S(2)}) copy-start(f32[16,2048]{1,0:T(8,128)} %get-tuple-element.5) | copy-start | bytes 393220
  298.3 196.6 %reduce-scatter.5.cloned.1.call-start = ((), (), s32[]{:S(2)}) async-start(), calls=%async_computation.3 | async-start | bytes 3538944 | tf_op jit(solution)/shard_map/reduce_scatter | solution.py:65
Sparse Core Ops, SparseCore 0:
  19.9 73.3 all-reduce.2
  298.4 73.5 reduce-scatter.2
  421.6 73.2 reduce-scatter.4
